TPU v7x, 16 devices: a whole 2x2x2 slice. The times are simulated.
16 devices in a mesh: rep: 1, dp: 16 (over x, y, z, core).
Axes of the slice: x: 2, y: 2, z: 2, core: 2. Of those that a mesh axis runs over, the one named last changes fastest.
Arguments:
- x: bfloat16 [16, 2048, 1152], P(('rep', 'dp'))
- dy: bfloat16 [16, 2048, 1152], P(('rep', 'dp'))
- w_gate: bfloat16 [2, 1152, 4608], P(None, 'dp')
- w_up: bfloat16 [2, 1152, 4608], P(None, 'dp')
- w_down: bfloat16 [2, 4608, 1152], P(None, 'dp')
Outputs:
- output 1: bfloat16 [16, 2048, 1152], P(('rep', 'dp'))
- output 2: bfloat16 [2, 1152, 4608], P('rep', 'dp')
- output 3: bfloat16 [2, 1152, 4608], P('rep', 'dp')
- output 4: bfloat16 [2, 4608, 1152], P('rep', 'dp')
All inputs are finite; a program needn't handle non-finite values.
Results may differ from a plain program's by a relative error of at most 0.018.
Values are sent between devices in bfloat16 or wider.
A program may use at most 2 GiB of HBM per device.

v0:
```python
import jax
import jax.numpy as jnp
from jax import lax

NAMES = ("w_gate", "w_up", "w_down")


def matmul(a, w):
    return jnp.dot(a, w, preferred_element_type=jnp.float32).astype(jnp.bfloat16)


def normed(h):
    wide = h.astype(jnp.float32)
    scale = lax.rsqrt(jnp.mean(wide**2, -1, keepdims=True) + 1e-6)
    return (wide * scale).astype(jnp.bfloat16)


def layer(h, w):
    a = normed(h)
    gate = jnp.dot(a, w["w_gate"], preferred_element_type=jnp.float32)
    up = jnp.dot(a, w["w_up"], preferred_element_type=jnp.float32)
    return h + matmul((jax.nn.silu(gate) * up).astype(jnp.bfloat16), w["w_down"])


def stack(weights, h):
    for number in range(weights["w_gate"].shape[0]):
        h = layer(h, {name: w[number] for name, w in weights.items()})
    return h


def solution(mesh):
    groups = mesh.shape["rep"]

    def step(x, dy, *weights):
        shape = x.shape
        x, dy = (t.reshape(groups, -1, *t.shape[1:]) for t in (x, dy))

        def of_a_group(x, dy):
            _, back = jax.vjp(stack, dict(zip(NAMES, weights, strict=True)), x)
            by_weights, by_x = back(dy)
            return (by_x, *(by_weights[name] for name in NAMES))

        by_x, *by_weights = jax.vmap(of_a_group)(x, dy)
        return (by_x.reshape(shape), *(t.reshape(-1, *t.shape[2:]) for t in by_weights))

    return step
```

profile of v0, /device:TPU:0, one launch (start us, length us, event | category | flops | bytes accessed | tf_op | source)
XLA Modules:
  0.0 2533.6 jit_solution(3336792527401903131)
XLA Ops:
  44.2 198.5 %while.13 = (bf16[1,2048,1152]{2,1,0:T(8,128)(2,1)}, bf16[1,288,1152]{2,1,0:T(8,128)(2,1)S(1)}, bf16[1,2048,4608]{1,2,0:T(8,128)(2,1)}, bf16[1,288,1152]{2,1,0:T...) while((bf16[1,2048,1152]{2,1,0:T(8,128)(2,1)}, ...), condition=%wide.windowed_dot_general_cond_ag, body=%wide.windowed_dot_general_body_ag.sunk | while | flops 5437145088 | bytes 36864540 | solution.py:9
  56.6 14.1 collective-permute-done
  95.6 13.3 collective-permute-start.2
  163.4 14.5 collective-permute-done.2
  223.4 13.2 collective-permute-start.3
  242.7 23.5 copy.2
  266.2 32.0 %fusion.194 = f32[2048,4608]{1,0:T(8,128)} fusion(bf16[1,1152,4608]{2,1,0:T(8,128)(2,1)} %all-gather.27.cloned.1.call-done, bf16[1,2048,1152]{1,2,0:T(8,128)(2,1)} %fusion.201), kind=kOutput, calls=%fused_computation.247 | convolution fusion | flops 21743271936 | bytes 53084160 | tf_op jit(solution)/vmap(jvp())/dot_general | solution.py:20
  298.2 45.3 %fusion.176 = (bf16[1,2048,4608]{2,1,0:T(8,128)(2,1)}, f32[2048,4608]{1,0:T(8,128)}) fusion(f32[2048,4608]{1,0:T(8,128)} %fusion.194, bf16[1,1152,4608]{2,1,0:T(8,128)(2,1)} %all-gather.29.cloned.1.call-done, bf16[1,2048,1152]{1,2,0:T(8,128)(2,1)} %fusion.201), kind=kOutput, calls=%fused_computation.215 | convolution fusion | flops 21799895040 | bytes 109707264 | tf_op jit(solution)/vmap(jvp())/dot_general | solution.py:21
  343.5 22.7 copy.6
  366.2 30.7 %fusion.203 = (f32[2048]{0:T(1024)S(1)}, bf16[1,2048,1152]{1,2,0:T(8,128)(2,1)}) fusion(bf16[1,2048,1152]{1,2,0:T(8,128)(2,1)} %copy.1, bf16[1,4608,1152]{2,1,0:T(8,128)(2,1)} %all-gather.31.cloned.1.call-done, bf16[1,2048,4608]{2,1,0:T(8,128)(2,1)} %get-tuple-element.281), kind=kOutput, calls=%fused_computation.256 | convolution fusion | flops 21755066368 | bytes 38936576 | tf_op jit(solution)/vmap(jvp())/dot_general | solution.py:9
  404.2 31.9 %fusion.186 = f32[2048,4608]{1,0:T(8,128)} fusion(bf16[1,1152,4608]{2,1,0:T(8,128)(2,1)} %all-gather.33.cloned.1.call-done, bf16[1,2048,1152]{1,2,0:T(8,128)(2,1)} %fusion.204), kind=kOutput, calls=%fused_computation.239 | convolution fusion | flops 21743271936 | bytes 53084160 | tf_op jit(solution)/vmap(jvp())/dot_general | solution.py:20
  436.1 45.8 %fusion.170 = (bf16[1,2048,4608]{2,1,0:T(8,128)(2,1)}, f32[2048,4608]{1,0:T(8,128)}) fusion(f32[2048,4608]{1,0:T(8,128)} %fusion.186, bf16[1,1152,4608]{2,1,0:T(8,128)(2,1)} %all-gather.35.cloned.1.call-done, bf16[1,2048,1152]{1,2,0:T(8,128)(2,1)} %fusion.204), kind=kOutput, calls=%fused_computation.205 | convolution fusion | flops 21799895040 | bytes 109707264 | tf_op jit(solution)/vmap(jvp())/dot_general | solution.py:21
  481.9 23.9 copy.4
  505.8 285.4 %while.18 = (bf16[1,2048,4608]{1,2,0:T(8,128)(2,1)}, bf16[1,2048,1152]{2,1,0:T(8,128)(2,1)}, f32[288,1152]{1,0:T(8,128)S(1)}, f32[288,1152]{1,0:T(8,128)}, u32[]...) while((bf16[1,2048,4608]{1,2,0:T(8,128)(2,1)}, ...), condition=%wide.windowed_dot_general_cond_rs.4.clone, body=%wide.windowed_dot_general_body_rs.4.clone.sunk | while | flops 5447245824 | bytes 94962248 | solution.py:9
  533.8 22.7 collective-permute-start.22
  605.3 27.8 %collective-permute-start.22 = (f32[288,1152]{1,0:T(8,128)}, f32[288,1152]{1,0:T(8,128)S(1)}, u32[]{:S(2)}, u32[]{:S(2)}) collective-permute-start(f32[288,1152]{1,0:T(8,128)} %get-tuple-element.543), channel_id=45, source_target_pairs={{0,1},{1,2},{2,3},{3,4},{4,5},{5,6},{6,7},{7,8},{8,9},{9,10},{10,1... | collective-permute-start | bytes 3981320 | tf_op jit(solution)/vmap(transpose(jvp()))/dot_general | solution.py:9
  676.7 26.5 %collective-permute-start.22 = (f32[288,1152]{1,0:T(8,128)}, f32[288,1152]{1,0:T(8,128)S(1)}, u32[]{:S(2)}, u32[]{:S(2)}) collective-permute-start(f32[288,1152]{1,0:T(8,128)} %get-tuple-element.543), channel_id=45, source_target_pairs={{0,1},{1,2},{2,3},{3,4},{4,5},{5,6},{6,7},{7,8},{8,9},{9,10},{10,1... | collective-permute-start | bytes 3981320 | tf_op jit(solution)/vmap(transpose(jvp()))/dot_general | solution.py:9
  747.3 25.9 %collective-permute-start.22 = (f32[288,1152]{1,0:T(8,128)}, f32[288,1152]{1,0:T(8,128)S(1)}, u32[]{:S(2)}, u32[]{:S(2)}) collective-permute-start(f32[288,1152]{1,0:T(8,128)} %get-tuple-element.543), channel_id=45, source_target_pairs={{0,1},{1,2},{2,3},{3,4},{4,5},{5,6},{6,7},{7,8},{8,9},{9,10},{10,1... | collective-permute-start | bytes 3981320 | tf_op jit(solution)/vmap(transpose(jvp()))/dot_general | solution.py:9
  795.3 39.1 %fusion.161 = (bf16[1,2048,4608]{2,1,0:T(8,128)(2,1)S(1)}, bf16[1,2048,4608]{2,1,0:T(8,128)(2,1)}) fusion(f32[2048,4608]{1,0:T(8,128)} %fusion.186, f32[2048,4608]{1,0:T(8,128)} %get-tuple-element.290, bf16[1,2048,4608]{2,1,0:T(8,128)(2,1)} %copy.2), kind=kLoop, calls=%fused_computation.195 | loop fusion | flops 141557760 | bytes 132120576 | tf_op jit(solution)/vmap(transpose(jvp(jit(silu))))/add_any | solution.py:22
  834.4 36.1 %fusion.211 = bf16[2048,1152]{0,1:T(8,128)(2,1)} fusion(bf16[1,1152,4608]{2,1,0:T(8,128)(2,1)} %all-gather.35.cloned.1.call-done, bf16[1,2048,4608]{2,1,0:T(8,128)(2,1)} %get-tuple-element.694), kind=kOutput, calls=%fused_computation.260 | convolution fusion | flops 21743271936 | bytes 34209792 | tf_op jit(solution)/vmap(transpose(jvp()))/dot_general | solution.py:21
  870.6 27.0 %fusion.205 = (f32[2048]{0:T(1024)S(1)}, bf16[1,2048,1152]{1,2,0:T(8,128)(2,1)}) fusion(bf16[1,2048,1152]{1,2,0:T(8,128)(2,1)} %get-tuple-element.284, bf16[2048,1152]{0,1:T(8,128)(2,1)} %fusion.211, bf16[1,1152,4608]{2,1,0:T(8,128)(2,1)} %all-gather.33.cloned.1.call-done, bf16[1,2048,4608]{2,1,0:T(8,128)(2,1)S(1)} %get-tuple-element.622), kind=kOutput, calls=%fused_computation.258 | convolution fusion | flops 21755066368 | bytes 43655168 | tf_op jit(solution)/vmap(transpose(jvp()))/dot_general | solution.py:20
  915.7 292.5 %while.19 = (bf16[1,2048,1152]{2,1,0:T(8,128)(2,1)}, bf16[1,2048,4608]{1,2,0:T(8,128)(2,1)}, f32[1152,288]{0,1:T(8,128)S(1)}, f32[1152,288]{0,1:T(8,128)}, u32[]...) while((bf16[1,2048,1152]{2,1,0:T(8,128)(2,1)}, ...), condition=%wide.windowed_dot_general_cond_rs.5.clone, body=%wide.windowed_dot_general_body_rs.5.clone.sunk | while | flops 5447245824 | bytes 94962248 | solution.py:9
  940.4 27.2 %collective-permute-start.26 = (f32[1152,288]{0,1:T(8,128)}, f32[1152,288]{0,1:T(8,128)}, u32[]{:S(2)}, u32[]{:S(2)}) collective-permute-start(f32[1152,288]{0,1:T(8,128)} %get-tuple-element.552), channel_id=51, source_target_pairs={{0,1},{1,2},{2,3},{3,4},{4,5},{5,6},{6,7},{7,8},{8,9},{9,10},{10,1... | collective-permute-start | bytes 3981320 | tf_op jit(solution)/vmap(transpose(jvp()))/dot_general | solution.py:9
  988.5 24.1 collective-permute-start.24
  1032.1 15.0 collective-permute-start.26
  1091.9 26.5 %collective-permute-start.26 = (f32[1152,288]{0,1:T(8,128)}, f32[1152,288]{0,1:T(8,128)}, u32[]{:S(2)}, u32[]{:S(2)}) collective-permute-start(f32[1152,288]{0,1:T(8,128)} %get-tuple-element.552), channel_id=51, source_target_pairs={{0,1},{1,2},{2,3},{3,4},{4,5},{5,6},{6,7},{7,8},{8,9},{9,10},{10,1... | collective-permute-start | bytes 3981320 | tf_op jit(solution)/vmap(transpose(jvp()))/dot_general | solution.py:9
  1163.8 25.9 %collective-permute-start.26 = (f32[1152,288]{0,1:T(8,128)}, f32[1152,288]{0,1:T(8,128)}, u32[]{:S(2)}, u32[]{:S(2)}) collective-permute-start(f32[1152,288]{0,1:T(8,128)} %get-tuple-element.552), channel_id=51, source_target_pairs={{0,1},{1,2},{2,3},{3,4},{4,5},{5,6},{6,7},{7,8},{8,9},{9,10},{10,1... | collective-permute-start | bytes 3981320 | tf_op jit(solution)/vmap(transpose(jvp()))/dot_general | solution.py:9
  1210.8 294.0 %while.16 = (bf16[1,2048,4608]{2,1,0:T(8,128)(2,1)}, bf16[1,2048,1152]{1,2,0:T(8,128)(2,1)}, f32[4608,72]{0,1:T(8,128)S(1)}, f32[4608,72]{0,1:T(8,128)}, u32[]{:...) while((bf16[1,2048,4608]{2,1,0:T(8,128)(2,1)}, ...), condition=%wide.windowed_dot_general_cond_rs.2.clone, body=%wide.windowed_dot_general_body_rs.2.clone.sunk | while | flops 5440167936 | bytes 94962248 | solution.py:21
  1223.8 17.9 collective-permute-done.12
  1244.9 28.2 %collective-permute-start.14 = (f32[4608,72]{0,1:T(8,128)}, f32[4608,72]{0,1:T(8,128)S(1)}, u32[]{:S(2)}, u32[]{:S(2)}) collective-permute-start(f32[4608,72]{0,1:T(8,128)} %get-tuple-element.525), channel_id=33, source_target_pairs={{0,1},{1,2},{2,3},{3,4},{4,5},{5,6},{6,7},{7,8},{8,9},{9,10},{10,1... | collective-permute-start | bytes 3981320 | tf_op jit(solution)/vmap(transpose(jvp()))/dot_general | solution.py:21
  1316.9 27.4 %collective-permute-start.14 = (f32[4608,72]{0,1:T(8,128)}, f32[4608,72]{0,1:T(8,128)S(1)}, u32[]{:S(2)}, u32[]{:S(2)}) collective-permute-start(f32[4608,72]{0,1:T(8,128)} %get-tuple-element.525), channel_id=33, source_target_pairs={{0,1},{1,2},{2,3},{3,4},{4,5},{5,6},{6,7},{7,8},{8,9},{9,10},{10,1... | collective-permute-start | bytes 3981320 | tf_op jit(solution)/vmap(transpose(jvp()))/dot_general | solution.py:21
  1387.3 28.2 %collective-permute-start.14 = (f32[4608,72]{0,1:T(8,128)}, f32[4608,72]{0,1:T(8,128)S(1)}, u32[]{:S(2)}, u32[]{:S(2)}) collective-permute-start(f32[4608,72]{0,1:T(8,128)} %get-tuple-element.525), channel_id=33, source_target_pairs={{0,1},{1,2},{2,3},{3,4},{4,5},{5,6},{6,7},{7,8},{8,9},{9,10},{10,1... | collective-permute-start | bytes 3981320 | tf_op jit(solution)/vmap(transpose(jvp()))/dot_general | solution.py:21
  1458.5 28.2 %collective-permute-start.14 = (f32[4608,72]{0,1:T(8,128)}, f32[4608,72]{0,1:T(8,128)S(1)}, u32[]{:S(2)}, u32[]{:S(2)}) collective-permute-start(f32[4608,72]{0,1:T(8,128)} %get-tuple-element.525), channel_id=33, source_target_pairs={{0,1},{1,2},{2,3},{3,4},{4,5},{5,6},{6,7},{7,8},{8,9},{9,10},{10,1... | collective-permute-start | bytes 3981320 | tf_op jit(solution)/vmap(transpose(jvp()))/dot_general | solution.py:21
  1506.9 52.7 %fusion.163 = (bf16[1,2048,4608]{2,1,0:T(8,128)(2,1)}, bf16[1,2048,4608]{2,1,0:T(8,128)(2,1)}) fusion(f32[2048,4608]{1,0:T(8,128)} %fusion.194, f32[2048,4608]{1,0:T(8,128)} %get-tuple-element.282, bf16[1,4608,1152]{2,1,0:T(8,128)(2,1)} %all-gather.31.cloned.1.call-done, bf16[1,2048,1152]{1,2,0:T(8,128)(2,1)} %fusion.262), kind=kOutput, calls=%fused_computation.197 | convolution fusion | flops 21894266880 | bytes 128581632 | tf_op jit(solution)/vmap(transpose(jvp()))/dot_general | solution.py:9
  1559.6 280.1 %while.17 = (bf16[1,2048,4608]{2,1,0:T(8,128)(2,1)}, bf16[1,2048,1152]{1,2,0:T(8,128)(2,1)}, f32[4608,72]{0,1:T(8,128)S(1)}, f32[4608,72]{0,1:T(8,128)}, u32[]{:...) while((bf16[1,2048,4608]{2,1,0:T(8,128)(2,1)}, ...), condition=%wide.windowed_dot_general_cond_rs.3.clone, body=%wide.windowed_dot_general_body_rs.3.clone.sunk | while | flops 5440167936 | bytes 94962248 | solution.py:21
  1584.0 27.2 %collective-permute-start.18 = (f32[4608,72]{0,1:T(8,128)}, f32[4608,72]{0,1:T(8,128)}, u32[]{:S(2)}, u32[]{:S(2)}) collective-permute-start(f32[4608,72]{0,1:T(8,128)} %get-tuple-element.534), channel_id=39, source_target_pairs={{0,1},{1,2},{2,3},{3,4},{4,5},{5,6},{6,7},{7,8},{8,9},{9,10},{10,1... | collective-permute-start | bytes 3981320 | tf_op jit(solution)/vmap(transpose(jvp()))/dot_general | solution.py:21
  1632.2 13.6 collective-permute-start.16
  1665.4 14.9 collective-permute-start.18
  1701.3 15.2 collective-permute-start.16
  1736.1 14.6 collective-permute-start.18
  1771.7 14.9 collective-permute-start.16
  1806.3 14.9 collective-permute-start.18
  1840.8 281.3 %while.14 = (bf16[1,2048,4608]{2,1,0:T(8,128)(2,1)}, bf16[1,2048,1152]{1,2,0:T(8,128)(2,1)}, f32[4608,72]{0,1:T(8,128)S(1)}, f32[4608,72]{0,1:T(8,128)}, u32[]{:...) while((bf16[1,2048,4608]{2,1,0:T(8,128)(2,1)}, ...), condition=%wide.windowed_dot_general_cond_rs.clone, body=%wide.windowed_dot_general_body_rs.clone.sunk | while | flops 5440167936 | bytes 94962248 | solution.py:20
  1842.2 14.9 collective-permute-start.4
  1876.8 14.9 collective-permute-start.6
  1912.8 15.0 collective-permute-start.4
  1947.5 14.9 collective-permute-start.6
  1983.5 14.9 collective-permute-start.4
  2018.1 14.9 collective-permute-start.6
  2054.0 14.9 collective-permute-start.4
  2088.7 14.9 collective-permute-start.6
  2123.2 278.4 %while.15 = (bf16[1,2048,4608]{2,1,0:T(8,128)(2,1)}, bf16[1,2048,1152]{1,2,0:T(8,128)(2,1)}, f32[4608,72]{0,1:T(8,128)S(1)}, f32[4608,72]{0,1:T(8,128)}, u32[]{:...) while((bf16[1,2048,4608]{2,1,0:T(8,128)(2,1)}, ...), condition=%wide.windowed_dot_general_cond_rs.1.clone, body=%wide.windowed_dot_general_body_rs.1.clone.sunk | while | flops 5440167936 | bytes 100270696 | solution.py:20
  2124.4 14.9 collective-permute-start.8
  2157.5 15.0 collective-permute-start.10
  2193.6 16.0 collective-permute-start.8
  2227.8 14.9 collective-permute-start.10
  2263.7 16.0 collective-permute-start.8
  2298.0 15.0 collective-permute-start.10
  2334.0 16.0 collective-permute-start.8
  2368.2 14.9 collective-permute-start.10
  2401.7 16.0 collective-permute-start.32
  2417.7 29.4 %fusion.221 = bf16[2048,1152]{0,1:T(8,128)(2,1)} fusion(bf16[1,1152,4608]{2,1,0:T(8,128)(2,1)} %all-gather.29.cloned.1.call-done, bf16[1,2048,4608]{2,1,0:T(8,128)(2,1)} %get-tuple-element.808), kind=kOutput, calls=%fused_computation.262 | convolution fusion | flops 21743271936 | bytes 34209792 | tf_op jit(solution)/vmap(transpose(jvp()))/dot_general | solution.py:21
  2447.2 26.9 %fusion.202 = (f32[2048]{0:T(1024)S(1)}, bf16[1,2048,1152]{1,2,0:T(8,128)(2,1)}) fusion(bf16[1,2048,1152]{1,2,0:T(8,128)(2,1)} %copy.1, bf16[2048,1152]{0,1:T(8,128)(2,1)} %fusion.221, bf16[1,1152,4608]{2,1,0:T(8,128)(2,1)} %all-gather.27.cloned.1.call-done, bf16[1,2048,4608]{2,1,0:T(8,128)(2,1)S(1)} %bitcast.610), kind=kOutput, calls=%fused_computation.255 | convolution fusion | flops 21755066368 | bytes 43655168 | tf_op jit(solution)/vmap(transpose(jvp()))/dot_general | solution.py:20
  2511.2 14.0 collective-permute-done.30
  (491 shorter events, 1255.6 us)
Async XLA Ops:
  7.2 259.0 %all-gather.27.cloned.1.call-start = ((), (), s32[]{:S(2)}) async-start(), calls=%async_computation | async-start | bytes 11280384 | tf_op jit(solution)/vmap(jvp())/squeeze | solution.py:27
  9.8 288.4 %all-gather.29.cloned.1.call-start = ((), (), s32[]{:S(2)}) async-start(), calls=%async_computation.1 | async-start | bytes 11280384 | tf_op jit(solution)/vmap(jvp())/squeeze | solution.py:27
  11.0 355.1 %all-gather.31.cloned.1.call-start = ((), (), s32[]{:S(2)}) async-start(), calls=%async_computation.2 | async-start | bytes 11280384 | tf_op jit(solution)/vmap(jvp())/squeeze | solution.py:27
  12.6 391.7 %all-gather.33.cloned.1.call-start = ((), (), s32[]{:S(2)}) async-start(), calls=%async_computation.3 | async-start | bytes 11280384 | tf_op jit(solution)/vmap(jvp())/squeeze | solution.py:27
  13.1 422.9 %all-gather.35.cloned.1.call-start = ((), (), s32[]{:S(2)}) async-start(), calls=%async_computation.4 | async-start | bytes 11280384 | tf_op jit(solution)/vmap(jvp())/squeeze | solution.py:27
  13.2 24.4 collective-permute-start.28
  44.2 26.5 %collective-permute-start = (bf16[1,288,1152]{2,1,0:T(8,128)(2,1)S(1)}, bf16[1,288,1152]{2,1,0:T(8,128)(2,1)}, u32[]{:S(2)}, u32[]{:S(2)}) collective-permute-start(bf16[1,288,1152]{2,1,0:T(8,128)(2,1)S(1)} %get-tuple-element.567), channel_id=7, source_target_pairs={{0,15},{1,0},{2,1},{3,2},{4,3},{5,4},{6,5},{7,6},{8,7},{9,8},{10,9... | collective-permute-start | bytes 1990664 | tf_op jit(solution)/vmap(transpose(jvp()))/dot_general | solution.py:9
  48.5 25.9 %collective-permute-start.2 = (bf16[1,288,1152]{2,1,0:T(8,128)(2,1)}, bf16[1,288,1152]{2,1,0:T(8,128)(2,1)}, u32[]{:S(2)}, u32[]{:S(2)}) collective-permute-start(bf16[1,288,1152]{2,1,0:T(8,128)(2,1)} %get-tuple-element.569), channel_id=8, source_target_pairs={{0,1},{1,2},{2,3},{3,4},{4,5},{5,6},{6,7},{7,8},{8,9},{9,10},{10,1... | collective-permute-start | bytes 1990664 | tf_op jit(solution)/vmap(transpose(jvp()))/dot_general | solution.py:9
  70.7 20.5 collective-permute-start.1
  92.4 24.5 collective-permute-start
  95.6 26.4 %collective-permute-start.2 = (bf16[1,288,1152]{2,1,0:T(8,128)(2,1)}, bf16[1,288,1152]{2,1,0:T(8,128)(2,1)}, u32[]{:S(2)}, u32[]{:S(2)}) collective-permute-start(bf16[1,288,1152]{2,1,0:T(8,128)(2,1)} %get-tuple-element.569), channel_id=8, source_target_pairs={{0,1},{1,2},{2,3},{3,4},{4,5},{5,6},{6,7},{7,8},{8,9},{9,10},{10,1... | collective-permute-start | bytes 1990664 | tf_op jit(solution)/vmap(transpose(jvp()))/dot_general | solution.py:9
  116.9 22.4 collective-permute-start.1
  144.5 33.5 %collective-permute-start.2 = (bf16[1,288,1152]{2,1,0:T(8,128)(2,1)}, bf16[1,288,1152]{2,1,0:T(8,128)(2,1)}, u32[]{:S(2)}, u32[]{:S(2)}) collective-permute-start(bf16[1,288,1152]{2,1,0:T(8,128)(2,1)} %get-tuple-element.569), channel_id=8, source_target_pairs={{0,1},{1,2},{2,3},{3,4},{4,5},{5,6},{6,7},{7,8},{8,9},{9,10},{10,1... | collective-permute-start | bytes 1990664 | tf_op jit(solution)/vmap(transpose(jvp()))/dot_general | solution.py:9
  159.0 32.1 %collective-permute-start.1 = (bf16[1,288,1152]{2,1,0:T(8,128)(2,1)}, bf16[1,288,1152]{2,1,0:T(8,128)(2,1)S(1)}, u32[]{:S(2)}, u32[]{:S(2)}) collective-permute-start(bf16[1,288,1152]{2,1,0:T(8,128)(2,1)} %collective-permute-done), channel_id=9, source_target_pairs={{0,15},{1,0},{2,1},{3,2},{4,3},{5,4},{6,5},{7,6},{8,7},{9,8},{10,9... | collective-permute-start | bytes 1990664 | tf_op jit(solution)/vmap(transpose(jvp()))/dot_general | solution.py:9
  197.3 20.1 collective-permute-start.2
  210.2 28.5 %collective-permute-start.1 = (bf16[1,288,1152]{2,1,0:T(8,128)(2,1)}, bf16[1,288,1152]{2,1,0:T(8,128)(2,1)S(1)}, u32[]{:S(2)}, u32[]{:S(2)}) collective-permute-start(bf16[1,288,1152]{2,1,0:T(8,128)(2,1)} %collective-permute-done), channel_id=9, source_target_pairs={{0,15},{1,0},{2,1},{3,2},{4,3},{5,4},{6,5},{7,6},{8,7},{9,8},{10,9... | collective-permute-start | bytes 1990664 | tf_op jit(solution)/vmap(transpose(jvp()))/dot_general | solution.py:9
  223.4 19.3 collective-permute-start.3
  533.8 29.0 %collective-permute-start.22 = (f32[288,1152]{1,0:T(8,128)}, f32[288,1152]{1,0:T(8,128)S(1)}, u32[]{:S(2)}, u32[]{:S(2)}) collective-permute-start(f32[288,1152]{1,0:T(8,128)} %get-tuple-element.543), channel_id=45, source_target_pairs={{0,1},{1,2},{2,3},{3,4},{4,5},{5,6},{6,7},{7,8},{8,9},{9,10},{10,1... | collective-permute-start | bytes 3981320 | tf_op jit(solution)/vmap(transpose(jvp()))/dot_general | solution.py:9
  576.0 19.2 collective-permute-start.20
  605.3 34.1 %collective-permute-start.22 = (f32[288,1152]{1,0:T(8,128)}, f32[288,1152]{1,0:T(8,128)S(1)}, u32[]{:S(2)}, u32[]{:S(2)}) collective-permute-start(f32[288,1152]{1,0:T(8,128)} %get-tuple-element.543), channel_id=45, source_target_pairs={{0,1},{1,2},{2,3},{3,4},{4,5},{5,6},{6,7},{7,8},{8,9},{9,10},{10,1... | collective-permute-start | bytes 3981320 | tf_op jit(solution)/vmap(transpose(jvp()))/dot_general | solution.py:9
  652.5 19.3 collective-permute-start.20
  676.7 32.8 %collective-permute-start.22 = (f32[288,1152]{1,0:T(8,128)}, f32[288,1152]{1,0:T(8,128)S(1)}, u32[]{:S(2)}, u32[]{:S(2)}) collective-permute-start(f32[288,1152]{1,0:T(8,128)} %get-tuple-element.543), channel_id=45, source_target_pairs={{0,1},{1,2},{2,3},{3,4},{4,5},{5,6},{6,7},{7,8},{8,9},{9,10},{10,1... | collective-permute-start | bytes 3981320 | tf_op jit(solution)/vmap(transpose(jvp()))/dot_general | solution.py:9
  722.6 19.3 collective-permute-start.20
  747.3 32.2 %collective-permute-start.22 = (f32[288,1152]{1,0:T(8,128)}, f32[288,1152]{1,0:T(8,128)S(1)}, u32[]{:S(2)}, u32[]{:S(2)}) collective-permute-start(f32[288,1152]{1,0:T(8,128)} %get-tuple-element.543), channel_id=45, source_target_pairs={{0,1},{1,2},{2,3},{3,4},{4,5},{5,6},{6,7},{7,8},{8,9},{9,10},{10,1... | collective-permute-start | bytes 3981320 | tf_op jit(solution)/vmap(transpose(jvp()))/dot_general | solution.py:9
  791.2 1707.2 %collective-permute-start.33 = (f32[288,1152]{1,0:T(8,128)}, f32[288,1152]{1,0:T(8,128)}, u32[]{:S(2)}, u32[]{:S(2)}) collective-permute-start(f32[288,1152]{1,0:T(8,128)} %get-tuple-element.52), channel_id=46, source_target_pairs={{0,1},{1,2},{2,3},{3,4},{4,5},{5,6},{6,7},{7,8},{8,9},{9,10},{10,1... | collective-permute-start | bytes 3981320 | tf_op jit(solution)/vmap(transpose(jvp()))/dot_general | solution.py:9
  940.4 33.5 %collective-permute-start.26 = (f32[1152,288]{0,1:T(8,128)}, f32[1152,288]{0,1:T(8,128)}, u32[]{:S(2)}, u32[]{:S(2)}) collective-permute-start(f32[1152,288]{0,1:T(8,128)} %get-tuple-element.552), channel_id=51, source_target_pairs={{0,1},{1,2},{2,3},{3,4},{4,5},{5,6},{6,7},{7,8},{8,9},{9,10},{10,1... | collective-permute-start | bytes 3981320 | tf_op jit(solution)/vmap(transpose(jvp()))/dot_general | solution.py:9
  988.5 31.5 %collective-permute-start.24 = (f32[1152,288]{0,1:T(8,128)}, f32[1152,288]{0,1:T(8,128)}, u32[]{:S(2)}, u32[]{:S(2)}) collective-permute-start(f32[1152,288]{0,1:T(8,128)} %broadcast_select_fusion.34), channel_id=49, source_target_pairs={{0,1},{1,2},{2,3},{3,4},{4,5},{5,6},{6,7},{7,8},{8,9},{9,10},{10,1... | collective-permute-start | bytes 3981320 | tf_op jit(solution)/vmap(transpose(jvp()))/dot_general | solution.py:9
  1032.1 21.3 collective-permute-start.26
  1091.9 32.8 %collective-permute-start.26 = (f32[1152,288]{0,1:T(8,128)}, f32[1152,288]{0,1:T(8,128)}, u32[]{:S(2)}, u32[]{:S(2)}) collective-permute-start(f32[1152,288]{0,1:T(8,128)} %get-tuple-element.552), channel_id=51, source_target_pairs={{0,1},{1,2},{2,3},{3,4},{4,5},{5,6},{6,7},{7,8},{8,9},{9,10},{10,1... | collective-permute-start | bytes 3981320 | tf_op jit(solution)/vmap(transpose(jvp()))/dot_general | solution.py:9
  1163.8 32.2 %collective-permute-start.26 = (f32[1152,288]{0,1:T(8,128)}, f32[1152,288]{0,1:T(8,128)}, u32[]{:S(2)}, u32[]{:S(2)}) collective-permute-start(f32[1152,288]{0,1:T(8,128)} %get-tuple-element.552), channel_id=51, source_target_pairs={{0,1},{1,2},{2,3},{3,4},{4,5},{5,6},{6,7},{7,8},{8,9},{9,10},{10,1... | collective-permute-start | bytes 3981320 | tf_op jit(solution)/vmap(transpose(jvp()))/dot_general | solution.py:9
  1208.2 1293.1 %collective-permute-start.34 = (f32[1152,288]{0,1:T(8,128)}, f32[1152,288]{0,1:T(8,128)}, u32[]{:S(2)}, u32[]{:S(2)}) collective-permute-start(f32[1152,288]{0,1:T(8,128)} %get-tuple-element.54), channel_id=52, source_target_pairs={{0,1},{1,2},{2,3},{3,4},{4,5},{5,6},{6,7},{7,8},{8,9},{9,10},{10,1... | collective-permute-start | bytes 3981320 | tf_op jit(solution)/vmap(transpose(jvp()))/dot_general | solution.py:9
  1212.0 29.7 %collective-permute-start.12 = (f32[4608,72]{0,1:T(8,128)}, f32[4608,72]{0,1:T(8,128)}, u32[]{:S(2)}, u32[]{:S(2)}) collective-permute-start(f32[4608,72]{0,1:T(8,128)} %broadcast_select_fusion.28), channel_id=31, source_target_pairs={{0,1},{1,2},{2,3},{3,4},{4,5},{5,6},{6,7},{7,8},{8,9},{9,10},{10,1... | collective-permute-start | bytes 3981320 | tf_op jit(solution)/vmap(transpose(jvp()))/dot_general | solution.py:21
  1214.6 27.1 %collective-permute-start.13 = (f32[4608,72]{0,1:T(8,128)S(1)}, f32[4608,72]{0,1:T(8,128)}, u32[]{:S(2)}, u32[]{:S(2)}) collective-permute-start(f32[4608,72]{0,1:T(8,128)S(1)} %broadcast_select_fusion.29), channel_id=30, source_target_pairs={{0,15},{1,0},{2,1},{3,2},{4,3},{5,4},{6,5},{7,6},{8,7},{9,8},{10,9... | collective-permute-start | bytes 3981320 | tf_op jit(solution)/vmap(transpose(jvp()))/dot_general | solution.py:21
  1244.9 36.3 %collective-permute-start.14 = (f32[4608,72]{0,1:T(8,128)}, f32[4608,72]{0,1:T(8,128)S(1)}, u32[]{:S(2)}, u32[]{:S(2)}) collective-permute-start(f32[4608,72]{0,1:T(8,128)} %get-tuple-element.525), channel_id=33, source_target_pairs={{0,1},{1,2},{2,3},{3,4},{4,5},{5,6},{6,7},{7,8},{8,9},{9,10},{10,1... | collective-permute-start | bytes 3981320 | tf_op jit(solution)/vmap(transpose(jvp()))/dot_general | solution.py:21
  1316.9 35.5 %collective-permute-start.14 = (f32[4608,72]{0,1:T(8,128)}, f32[4608,72]{0,1:T(8,128)S(1)}, u32[]{:S(2)}, u32[]{:S(2)}) collective-permute-start(f32[4608,72]{0,1:T(8,128)} %get-tuple-element.525), channel_id=33, source_target_pairs={{0,1},{1,2},{2,3},{3,4},{4,5},{5,6},{6,7},{7,8},{8,9},{9,10},{10,1... | collective-permute-start | bytes 3981320 | tf_op jit(solution)/vmap(transpose(jvp()))/dot_general | solution.py:21
  1387.3 36.3 %collective-permute-start.14 = (f32[4608,72]{0,1:T(8,128)}, f32[4608,72]{0,1:T(8,128)S(1)}, u32[]{:S(2)}, u32[]{:S(2)}) collective-permute-start(f32[4608,72]{0,1:T(8,128)} %get-tuple-element.525), channel_id=33, source_target_pairs={{0,1},{1,2},{2,3},{3,4},{4,5},{5,6},{6,7},{7,8},{8,9},{9,10},{10,1... | collective-permute-start | bytes 3981320 | tf_op jit(solution)/vmap(transpose(jvp()))/dot_general | solution.py:21
  1436.1 19.2 collective-permute-start.12
  1458.5 36.3 %collective-permute-start.14 = (f32[4608,72]{0,1:T(8,128)}, f32[4608,72]{0,1:T(8,128)S(1)}, u32[]{:S(2)}, u32[]{:S(2)}) collective-permute-start(f32[4608,72]{0,1:T(8,128)} %get-tuple-element.525), channel_id=33, source_target_pairs={{0,1},{1,2},{2,3},{3,4},{4,5},{5,6},{6,7},{7,8},{8,9},{9,10},{10,1... | collective-permute-start | bytes 3981320 | tf_op jit(solution)/vmap(transpose(jvp()))/dot_general | solution.py:21
  1504.8 990.5 %collective-permute-start.31 = (f32[4608,72]{0,1:T(8,128)}, f32[4608,72]{0,1:T(8,128)}, u32[]{:S(2)}, u32[]{:S(2)}) collective-permute-start(f32[4608,72]{0,1:T(8,128)} %get-tuple-element.48), channel_id=34, source_target_pairs={{0,1},{1,2},{2,3},{3,4},{4,5},{5,6},{6,7},{7,8},{8,9},{9,10},{10,1... | collective-permute-start | bytes 3981320 | tf_op jit(solution)/vmap(transpose(jvp()))/dot_general | solution.py:21
  1584.0 35.4 %collective-permute-start.18 = (f32[4608,72]{0,1:T(8,128)}, f32[4608,72]{0,1:T(8,128)}, u32[]{:S(2)}, u32[]{:S(2)}) collective-permute-start(f32[4608,72]{0,1:T(8,128)} %get-tuple-element.534), channel_id=39, source_target_pairs={{0,1},{1,2},{2,3},{3,4},{4,5},{5,6},{6,7},{7,8},{8,9},{9,10},{10,1... | collective-permute-start | bytes 3981320 | tf_op jit(solution)/vmap(transpose(jvp()))/dot_general | solution.py:21
  1632.2 22.9 collective-permute-start.16
  1665.4 23.1 collective-permute-start.18
  1701.3 24.5 collective-permute-start.16
  1736.1 22.8 collective-permute-start.18
  1771.7 24.2 collective-permute-start.16
  1806.3 23.1 collective-permute-start.18
  1842.2 24.3 collective-permute-start.4
  1876.8 23.0 collective-permute-start.6
  1912.8 24.4 collective-permute-start.4
  1947.5 23.0 collective-permute-start.6
  1983.5 24.3 collective-permute-start.4
  2018.1 23.0 collective-permute-start.6
  2054.0 24.3 collective-permute-start.4
  2088.7 23.0 collective-permute-start.6
  2124.4 23.3 collective-permute-start.8
  2157.5 23.2 collective-permute-start.10
  2193.6 24.3 collective-permute-start.8
  2227.8 23.1 collective-permute-start.10
  2263.7 24.3 collective-permute-start.8
  2298.0 23.2 collective-permute-start.10
  2334.0 24.3 collective-permute-start.8
  2368.2 23.1 collective-permute-start.10
  2401.7 95.3 %collective-permute-start.32 = (f32[4608,72]{0,1:T(8,128)}, f32[4608,72]{0,1:T(8,128)}, u32[]{:S(2)}, u32[]{:S(2)}) collective-permute-start(f32[4608,72]{0,1:T(8,128)} %get-tuple-element.50), channel_id=40, source_target_pairs={{0,1},{1,2},{2,3},{3,4},{4,5},{5,6},{6,7},{7,8},{8,9},{9,10},{10,1... | collective-permute-start | bytes 3981320 | tf_op jit(solution)/vmap(transpose(jvp()))/dot_general | solution.py:21
  2495.3 30.0 %collective-permute-start.30 = (f32[4608,72]{0,1:T(8,128)}, f32[4608,72]{0,1:T(8,128)S(1)}, u32[]{:S(2)}, u32[]{:S(2)}) collective-permute-start(f32[4608,72]{0,1:T(8,128)} %get-tuple-element.46), channel_id=28, source_target_pairs={{0,1},{1,2},{2,3},{3,4},{4,5},{5,6},{6,7},{7,8},{8,9},{9,10},{10,1... | collective-permute-start | bytes 3981320 | tf_op jit(solution)/vmap(transpose(jvp()))/dot_general | solution.py:20
  (96 other events, 2371.7 us)
Sparse Core Ops, SparseCore 0:
  10.2 84.6 all-gather.26
  97.1 89.9 all-gather.28
  189.3 78.2 all-gather.30
  269.7 56.0 all-gather.32
  327.9 55.8 all-gather.34
where the time goes:
time: 2540 us; the launch traced here: 2530 us
  starting transfers between devices  864 us (34%)
  matrix products  765 us (30%)
  waiting for transfers between devices  452 us (18%)
  other arithmetic  301 us (12%)
  local copies, waits for them, and re-layouts  135 us (5%)
    dot_general x51, starting transfers between devices, matmul(): jnp.dot(a, w, preferred_element_type=jnp.float32).astype(jnp.bfloat16)  353 us
    dot_general x20, matrix products, layer(): up = jnp.dot(a, w['w_up'], preferred_element_type=jnp.float32)  287 us
    dot_general x34, starting transfers between devices, layer(): up = jnp.dot(a, w['w_up'], preferred_element_type=jnp.float32)  265 us
    dot_general x20, matrix products, layer(): gate = jnp.dot(a, w['w_gate'], preferred_element_type=jnp.float32)  248 us
    dot_general x34, starting transfers between devices, layer(): gate = jnp.dot(a, w['w_gate'], preferred_element_type=jnp.float32)  246 us
    dot_general x26, matrix products, matmul(): jnp.dot(a, w, preferred_element_type=jnp.float32).astype(jnp.bfloat16)  231 us
    dot_general x51, waiting for transfers between devices, matmul(): jnp.dot(a, w, preferred_element_type=jnp.float32).astype(jnp.bfloat16)  194 us
    dot_general x34, waiting for transfers between devices, layer(): gate = jnp.dot(a, w['w_gate'], preferred_element_type=jnp.float32)  132 us
  transfers between devices with their start and end apart: 124, of which 69 were waited for; matrix products, arithmetic and copies ran while one was open for 43% of the time, Pallas kernels for 0%

commit v1 on v0

v1 whole, which is shorter than its diff:
```python
import jax
import jax.numpy as jnp
from jax import lax
from jax.sharding import PartitionSpec as P

F32 = jnp.float32
BF16 = jnp.bfloat16


def mm(a, b, ca, cb):
    return lax.dot_general(a, b, (((ca,), (cb,)), ((), ())), preferred_element_type=F32)


def normed(h):
    wide = h.astype(F32)
    scale = lax.rsqrt(jnp.mean(wide**2, -1, keepdims=True) + 1e-6)
    return (wide * scale).astype(BF16), scale


def norm_back(h, scale, da, dh):
    wide = h.astype(F32)
    da = da.astype(F32)
    inner = jnp.mean(da * wide, -1, keepdims=True)
    return (dh.astype(F32) + scale * (da - wide * (scale * scale * inner))).astype(BF16)


def gather(w):
    return lax.all_gather(w, "dp", axis=0, tiled=True)


def scatter(dw):
    return lax.psum_scatter(dw, "dp", scatter_dimension=0, tiled=True)


def local(x, dy, w_gate, w_up, w_down):
    layers = w_gate.shape[0]
    h, dh = x[0], dy[0]
    wg = [gather(w_gate[n]) for n in range(layers)]
    wu = [gather(w_up[n]) for n in range(layers)]
    wd = [gather(w_down[n]) for n in range(layers)]
    saved = []
    for n in range(layers):
        a, scale = normed(h)
        gate = mm(a, wg[n], 1, 0)
        up = mm(a, wu[n], 1, 0)
        act = (jax.nn.silu(gate) * up).astype(BF16)
        saved.append((h, scale, a, gate, up, act))
        if n < layers - 1:
            h = h + mm(act, wd[n], 1, 0).astype(BF16)
    grads = [[None] * layers for _ in range(3)]
    for n in reversed(range(layers)):
        h, scale, a, gate, up, act = saved[n]
        grads[2][n] = scatter(mm(act, dh, 0, 0).astype(BF16))
        dact = mm(dh, wd[n], 1, 1).astype(BF16).astype(F32)
        s = jax.nn.sigmoid(gate)
        dup = (dact * (gate * s)).astype(BF16)
        dgate = (dact * up * (s * (1 + gate * (1 - s)))).astype(BF16)
        grads[0][n] = scatter(mm(a, dgate, 0, 0).astype(BF16))
        grads[1][n] = scatter(mm(a, dup, 0, 0).astype(BF16))
        da = mm(dgate, wg[n], 1, 1).astype(BF16).astype(F32) + mm(dup, wu[n], 1, 1).astype(BF16).astype(F32)
        dh = norm_back(h, scale, da, dh)
    return (dh[None], *(jnp.stack(g) for g in grads))


def solution(mesh):
    seq = P(("rep", "dp"), None, None)
    w = P(None, "dp", None)
    out = P("rep", "dp", None)
    return jax.shard_map(local, mesh=mesh, in_specs=(seq, seq, w, w, w), out_specs=(seq, out, out, out), check_vma=False)
```

time: 2540 us -> 1070 us (0.42)
  starting transfers between devices: 864 us -> 0.49 us
  other arithmetic: 301 us -> 38.5 us
  matrix products: 765 us -> 590 us
  local copies, waits for them, and re-layouts: 135 us -> 28.6 us
  waiting for transfers between devices: 452 us -> 391 us
    dot_general x119 -> x0, starting transfers between devices: 864 us -> none  [the longest x51 353 us: matmul(): jnp.dot(a, w, preferred_element_type=jnp.float32).astype(jnp.bfloat16)]
    dot_general x119 -> x0, waiting for transfers between devices: 452 us -> none  [the longest x51 194 us: matmul(): jnp.dot(a, w, preferred_element_type=jnp.float32).astype(jnp.bfloat16)]
    reduce_scatter x0 -> x6, waiting for transfers between devices: none -> 234 us  [scatter(): return lax.psum_scatter(dw, 'dp', scatter_dimension=0, tiled=True)]
    dot_general x96 -> x0, other arithmetic: 213 us -> none
    dot_general x66 -> x17, matrix products: 765 us -> 590 us  [mm(): lax.dot_general(a, b, (((ca,), (cb,)), ((), ())), preferred_element_type=...]
    all_gather x0 -> x6, waiting for transfers between devices: none -> 155 us  [gather(): return lax.all_gather(w, 'dp', axis=0, tiled=True)]
    add_any x3 -> x0, other arithmetic: 61.6 us -> none  [the longest x1 39.1 us: layer(): jax.nn.silu(gate) * up]
    unnamed x70 -> x31, local copies, waits for them, and re-layouts: 78 us -> 21.2 us
  transfers between devices with their start and end apart: 124 -> 12, of which waited for: 69 -> 9; matrix products, arithmetic and copies ran while one was open for 43% -> 46% of each run, Pallas kernels for 0% -> 0%
where the time goes in v1:
time: 1070 us; the launch traced here: 1060 us
  matrix products  590 us (55%)
  waiting for transfers between devices  391 us (37%)
  other arithmetic  38.5 us (4%)
  local copies, waits for them, and re-layouts  28.6 us (3%)
  between operations  14.7 us (1%)
    dot_general x17, matrix products, mm(): lax.dot_general(a, b, (((ca,), (cb,)), ((), ())), preferred_element_type=...  590 us
    reduce_scatter x6, waiting for transfers between devices, scatter(): return lax.psum_scatter(dw, 'dp', scatter_dimension=0, tiled=True)  234 us
    all_gather x6, waiting for transfers between devices, gather(): return lax.all_gather(w, 'dp', axis=0, tiled=True)  155 us
  transfers between devices with their start and end apart: 12, of which 9 were waited for; matrix products, arithmetic and copies ran while one was open for 46% of the time, Pallas kernels for 0%

profile of v1, /device:TPU:0, one launch (start us, length us, event | category | flops | bytes accessed | tf_op | source)
XLA Modules:
  0.0 1062.7 jit_solution(5394213057100286787)
XLA Ops:
  7.2 0.0 all-gather.13.cloned.1.call-start
  7.2 2.4 fusion.74
  9.6 0.0 all-gather.13.cloned.1.call-update
  9.7 0.0 all-gather.15.cloned.1.call-start
  9.7 2.5 fusion.73
  12.2 0.0 all-gather.15.cloned.1.call-update
  12.2 0.0 all-gather.17.cloned.1.call-start
  12.3 2.5 fusion.75
  14.7 0.0 all-gather.17.cloned.1.call-update
  14.8 0.0 all-gather.19.cloned.1.call-start
  14.8 0.5 all-gather.19.cloned.1.call-update
  15.4 0.0 all-gather.23.cloned.1.call-start
  15.4 0.5 all-gather.23.cloned.1.call-update
  15.9 0.0 all-gather.21.cloned.1.call-start
  16.0 0.5 all-gather.21.cloned.1.call-update
  16.5 0.0 reduce-scatter.15.cloned.1.call-start
  16.6 6.6 copy.10
  23.2 3.3 fusion.28
  26.5 0.6 copy-done.3
  27.1 6.7 copy.9
  33.8 35.7 %all-gather.13.cloned.1.call-done = bf16[1,1152,4608]{2,1,0:T(8,128)(2,1)} async-done(((bf16[1,72,4608]{2,1,0:T(8,128)(2,1)}), bf16[1,1152,4608]{2,1,0:T(8,128)(2,1)}) %all-gather.13.cloned.1.call-update) | async-done | bytes 10616848 | tf_op jit(solution)/shard_map/all_gather | solution.py:28
  69.5 32.0 %fusion.26 = f32[2048,4608]{1,0:T(8,128)} fusion(bf16[1,1152,4608]{2,1,0:T(8,128)(2,1)} %all-gather.13.cloned.1.call-done, bf16[1,2048,1152]{1,2,0:T(8,128)(2,1)} %copy.10, f32[2048]{0:T(1024)S(1)} %add_rsqrt_fusion.1), kind=kOutput, calls=%fused_computation.50 | convolution fusion | flops 21750349824 | bytes 53092352 | tf_op jit(solution)/shard_map/dot_general | solution.py:11
  101.6 26.1 %all-gather.15.cloned.1.call-done = bf16[1,1152,4608]{2,1,0:T(8,128)(2,1)} async-done(((bf16[1,72,4608]{2,1,0:T(8,128)(2,1)}), bf16[1,1152,4608]{2,1,0:T(8,128)(2,1)}) %all-gather.15.cloned.1.call-update) | async-done | bytes 10616848 | tf_op jit(solution)/shard_map/all_gather | solution.py:28
  127.7 46.0 %multiply_convert_fusion.1 = (bf16[2048,4608]{1,0:T(8,128)(2,1)}, f32[2048,4608]{1,0:T(8,128)}) fusion(f32[2048,4608]{1,0:T(8,128)} %fusion.26, bf16[1,1152,4608]{2,1,0:T(8,128)(2,1)} %all-gather.15.cloned.1.call-done, bf16[1,2048,1152]{1,2,0:T(8,128)(2,1)} %copy.10, f32[2048]{0:T(1024)S(1)} %add_rsqrt_fusion.1), kind=kOutput, calls=%fused_computation.13 | convolution fusion | flops 21806972928 | bytes 109715456 | tf_op jit(solution)/shard_map/dot_general | solution.py:11
  173.7 12.1 %all-gather.17.cloned.1.call-done = bf16[1,4608,1152]{2,1,0:T(8,128)(2,1)} async-done(((bf16[1,288,1152]{2,1,0:T(8,128)(2,1)}), bf16[1,4608,1152]{2,1,0:T(8,128)(2,1)}) %all-gather.17.cloned.1.call-update) | async-done | bytes 10616848 | tf_op jit(solution)/shard_map/all_gather | solution.py:28
  185.8 30.7 %fusion.35 = (f32[2048]{0:T(1024)S(1)}, bf16[2048,1152]{0,1:T(8,128)(2,1)}) fusion(bf16[2048,4608]{1,0:T(8,128)(2,1)} %get-tuple-element.18, bf16[1,4608,1152]{2,1,0:T(8,128)(2,1)} %all-gather.17.cloned.1.call-done, bf16[1,2048,1152]{1,2,0:T(8,128)(2,1)} %copy.10), kind=kOutput, calls=%fused_computation.59 | convolution fusion | flops 21755066368 | bytes 38936576 | tf_op jit(solution)/shard_map/dot_general | solution.py:11
  216.5 27.3 %all-gather.19.cloned.1.call-done = bf16[1,4608,1152]{2,1,0:T(8,128)(2,1)} async-done(((bf16[1,288,1152]{2,1,0:T(8,128)(2,1)}), bf16[1,4608,1152]{2,1,0:T(8,128)(2,1)}) %all-gather.19.cloned.1.call-update) | async-done | bytes 10616848 | tf_op jit(solution)/shard_map/all_gather | solution.py:28
  243.8 31.4 %convolution_convert_fusion.5 = bf16[2048,4608]{1,0:T(8,128)(2,1)} fusion(bf16[1,4608,1152]{2,1,0:T(8,128)(2,1)} %all-gather.19.cloned.1.call-done, bf16[1,2048,1152]{2,1,0:T(8,128)(2,1)} %param.6), kind=kOutput, calls=%fused_computation.21 | convolution fusion | flops 21752709120 | bytes 34209792 | tf_op jit(solution)/shard_map/dot_general | solution.py:11
  275.2 27.1 %all-gather.23.cloned.1.call-done = bf16[1,1152,4608]{2,1,0:T(8,128)(2,1)} async-done(((bf16[1,72,4608]{2,1,0:T(8,128)(2,1)}), bf16[1,1152,4608]{2,1,0:T(8,128)(2,1)}) %all-gather.23.cloned.1.call-update) | async-done | bytes 10616848 | tf_op jit(solution)/shard_map/all_gather | solution.py:28
  302.4 32.0 %fusion.10 = f32[2048,4608]{1,0:T(8,128)} fusion(bf16[1,1152,4608]{2,1,0:T(8,128)(2,1)} %all-gather.23.cloned.1.call-done, bf16[2048,1152]{0,1:T(8,128)(2,1)} %get-tuple-element.21, f32[2048]{0:T(1024)S(1)} %add_rsqrt_fusion), kind=kOutput, calls=%fused_computation.34 | convolution fusion | flops 21750349824 | bytes 53092352 | tf_op jit(solution)/shard_map/dot_general | solution.py:11
  334.3 26.6 %all-gather.21.cloned.1.call-done = bf16[1,1152,4608]{2,1,0:T(8,128)(2,1)} async-done(((bf16[1,72,4608]{2,1,0:T(8,128)(2,1)}), bf16[1,1152,4608]{2,1,0:T(8,128)(2,1)}) %all-gather.21.cloned.1.call-update) | async-done | bytes 10616848 | tf_op jit(solution)/shard_map/all_gather | solution.py:28
  360.9 60.2 %fusion.1 = (bf16[2048,4608]{1,0:T(8,128)(2,1)}, bf16[2048,4608]{1,0:T(8,128)(2,1)}, f32[2048,4608]{1,0:T(8,128)}) fusion(bf16[2048,4608]{1,0:T(8,128)(2,1)} %convolution_convert_fusion.5, f32[2048,4608]{1,0:T(8,128)} %fusion.10, bf16[1,1152,4608]{2,1,0:T(8,128)(2,1)} %all-gather.21.cloned.1.call-done, bf16[2048,1152]{0,1:T(8,128)(2,1)} %get-tuple-element.21, ...), kind=kOutput, calls=%fused_computation.5 | convolution fusion | flops 21882470400 | bytes 147464192 | tf_op jit(solution)/shard_map/dot_general | solution.py:11
  421.1 28.4 %fusion.54 = bf16[2048,1152]{0,1:T(8,128)(2,1)S(1)} fusion(bf16[2048,4608]{1,0:T(8,128)(2,1)} %get-tuple-element.10, bf16[1,1152,4608]{2,1,0:T(8,128)(2,1)} %all-gather.23.cloned.1.call-done), kind=kOutput, calls=%fused_computation.72 | convolution fusion | flops 21745631232 | bytes 34209792 | tf_op jit(solution)/shard_map/dot_general | solution.py:11
  449.6 32.0 %fusion.37 = (f32[2048]{0:T(1024)S(1)}, bf16[2048,1152]{0,1:T(8,128)(2,1)}) fusion(bf16[2048,1152]{0,1:T(8,128)(2,1)S(1)} %copy-done, bf16[2048,1152]{0,1:T(8,128)(2,1)S(1)} %fusion.54, bf16[2048,4608]{1,0:T(8,128)(2,1)} %get-tuple-element.11, bf16[1,1152,4608]{2,1,0:T(8,128)(2,1)} %all-gather.21.cloned.1.call-done), kind=kOutput, calls=%fused_computation.61 | convolution fusion | flops 21759784960 | bytes 43655168 | tf_op jit(solution)/shard_map/dot_general | solution.py:11
  481.6 13.8 %fusion.41 = bf16[2048,1152]{0,1:T(8,128)(2,1)} fusion(bf16[2048,1152]{0,1:T(8,128)(2,1)} %get-tuple-element.21, bf16[2048,1152]{0,1:T(8,128)(2,1)} %get-tuple-element.24, bf16[2048,1152]{0,1:T(8,128)(2,1)} %copy-done.2, bf16[1,2048,1152]{1,2,0:T(8,128)(2,1)} %copy.9, f32[2048]{0:T(1024)S(1)} %multiply_multiply_fusion.1, f32[2048]{0:T(1024)S(1)} %add_rsqrt_fusion), kind=kLoop, calls=%fused_computation.65 | loop fusion | flops 23592960 | bytes 23609344 | tf_op jit(solution)/shard_map/convert_element_type | solution.py:24
  495.4 30.9 %convolution_convert_fusion.7 = bf16[4608,1152]{1,0:T(8,128)(2,1)} fusion(bf16[2048,4608]{1,0:T(8,128)(2,1)} %get-tuple-element.18, bf16[2048,1152]{0,1:T(8,128)(2,1)} %fusion.41), kind=kOutput, calls=%fused_computation.23 | convolution fusion | flops 21748580352 | bytes 34209792 | tf_op jit(solution)/shard_map/dot_general | solution.py:11
  526.3 0.0 reduce-scatter.15.cloned.1.call-update
  526.3 0.0 reduce-scatter.17.cloned.1.call-start
  526.3 37.5 %convolution_convert_fusion.6 = bf16[4608,1152]{1,0:T(8,128)(2,1)} fusion(f32[2048,4608]{1,0:T(8,128)} %get-tuple-element.22, f32[2048,4608]{1,0:T(8,128)} %fusion.10, bf16[1,2048,1152]{2,1,0:T(8,128)(2,1)} %param.6), kind=kOutput, calls=%fused_computation.22 | convolution fusion | flops 21805203456 | bytes 90832896 | tf_op jit(solution)/shard_map/dot_general | solution.py:11
  563.8 0.0 reduce-scatter.17.cloned.1.call-update
  563.8 0.0 reduce-scatter.11.cloned.1.call-start
  563.9 53.0 %fusion.4 = (bf16[2048,4608]{1,0:T(8,128)(2,1)}, bf16[2048,4608]{1,0:T(8,128)(2,1)}) fusion(f32[2048,4608]{1,0:T(8,128)} %get-tuple-element.19, f32[2048,4608]{1,0:T(8,128)} %fusion.26, bf16[2048,1152]{0,1:T(8,128)(2,1)} %fusion.41, bf16[1,4608,1152]{2,1,0:T(8,128)(2,1)} %all-gather.17.cloned.1.call-done), kind=kOutput, calls=%fused_computation.8 | convolution fusion | flops 21884829696 | bytes 128581632 | tf_op jit(solution)/shard_map/dot_general | solution.py:11
  616.9 28.6 %convolution_convert_fusion.1 = bf16[1152,4608]{1,0:T(8,128)(2,1)} fusion(bf16[2048,4608]{1,0:T(8,128)(2,1)} %get-tuple-element.9, bf16[1,2048,1152]{1,2,0:T(8,128)(2,1)} %copy.10, f32[2048]{0:T(1024)S(1)} %copy-done.6), kind=kOutput, calls=%fused_computation.17 | convolution fusion | flops 21755658240 | bytes 34217984 | tf_op jit(solution)/shard_map/dot_general | solution.py:11
  645.5 0.0 reduce-scatter.11.cloned.1.call-update
  645.5 0.0 reduce-scatter.13.cloned.1.call-start
  645.6 0.6 copy-done.9
  646.2 28.7 %convolution_convert_fusion = bf16[1152,4608]{1,0:T(8,128)(2,1)} fusion(bf16[2048,4608]{1,0:T(8,128)(2,1)} %get-tuple-element.11, bf16[2048,1152]{0,1:T(8,128)(2,1)} %get-tuple-element.21, f32[2048]{0:T(1024)S(1)} %copy-done.9), kind=kOutput, calls=%fused_computation.16 | convolution fusion | flops 21755658240 | bytes 34217984 | tf_op jit(solution)/shard_map/dot_general | solution.py:11
  674.9 0.0 reduce-scatter.13.cloned.1.call-update
  674.9 0.0 reduce-scatter.7.cloned.1.call-start
  675.0 28.6 %convolution_convert_fusion.3 = bf16[1152,4608]{1,0:T(8,128)(2,1)} fusion(bf16[2048,4608]{1,0:T(8,128)(2,1)} %get-tuple-element.8, bf16[1,2048,1152]{1,2,0:T(8,128)(2,1)} %copy.10, f32[2048]{0:T(1024)S(1)} %copy-done.6), kind=kOutput, calls=%fused_computation.19 | convolution fusion | flops 21755658240 | bytes 34217984 | tf_op jit(solution)/shard_map/dot_general | solution.py:11
  703.5 0.0 reduce-scatter.7.cloned.1.call-update
  703.6 0.0 reduce-scatter.9.cloned.1.call-start
  703.6 28.9 %convolution_convert_fusion.2 = bf16[1152,4608]{1,0:T(8,128)(2,1)} fusion(bf16[2048,4608]{1,0:T(8,128)(2,1)} %get-tuple-element.10, bf16[2048,1152]{0,1:T(8,128)(2,1)} %get-tuple-element.21, f32[2048]{0:T(1024)S(1)} %copy-done.9), kind=kOutput, calls=%fused_computation.18 | convolution fusion | flops 21755658240 | bytes 34217984 | tf_op jit(solution)/shard_map/dot_general | solution.py:11
  732.5 0.0 reduce-scatter.9.cloned.1.call-update
  732.5 28.5 %fusion.42 = bf16[2048,1152]{0,1:T(8,128)(2,1)S(1)} fusion(bf16[2048,4608]{1,0:T(8,128)(2,1)} %get-tuple-element.8, bf16[1,1152,4608]{2,1,0:T(8,128)(2,1)} %all-gather.13.cloned.1.call-done), kind=kOutput, calls=%fused_computation.68 | convolution fusion | flops 21745631232 | bytes 34209792 | tf_op jit(solution)/shard_map/dot_general | solution.py:11
  761.0 32.2 %fusion.30 = (f32[2048]{0:T(1024)S(1)}, bf16[2048,1152]{0,1:T(8,128)(2,1)}) fusion(bf16[2048,1152]{0,1:T(8,128)(2,1)S(1)} %fusion.42, bf16[1,2048,1152]{1,2,0:T(8,128)(2,1)S(1)} %bitcast.94, bf16[2048,4608]{1,0:T(8,128)(2,1)} %get-tuple-element.9, bf16[1,1152,4608]{2,1,0:T(8,128)(2,1)} %all-gather.15.cloned.1.call-done), kind=kOutput, calls=%fused_computation.54 | convolution fusion | flops 21759784960 | bytes 43655168 | tf_op jit(solution)/shard_map/dot_general | solution.py:11
  793.3 13.9 %fusion.61 = bf16[1,2048,1152]{1,2,0:T(8,128)(2,1)} fusion(bf16[2048,1152]{0,1:T(8,128)(2,1)} %get-tuple-element.26, bf16[2048,1152]{0,1:T(8,128)(2,1)} %copy-done.1, bf16[2048,1152]{0,1:T(8,128)(2,1)} %fusion.41, bf16[1,2048,1152]{1,2,0:T(8,128)(2,1)} %copy.10, f32[2048]{0:T(1024)S(1)} %multiply_multiply_fusion, f32[2048]{0:T(1024)S(1)} %copy-done.7), kind=kLoop, calls=%fused_computation.74 | loop fusion | flops 23592960 | bytes 23609344 | tf_op jit(solution)/shard_map/broadcast_in_dim | solution.py:62
  807.2 6.6 copy.11
  813.8 2.5 pad_maximum_fusion.2
  816.3 59.6 %reduce-scatter.13.cloned.1.call-done = bf16[72,4608]{1,0:T(8,128)(2,1)} async-done(((bf16[1152,4608]{1,0:T(8,128)(2,1)}), bf16[72,4608]{1,0:T(8,128)(2,1)}) %reduce-scatter.13.cloned.1.call-update) | async-done | bytes 663568 | tf_op jit(solution)/shard_map/reduce_scatter | solution.py:32
  875.9 2.5 pad_maximum_fusion.1
  878.4 86.2 %reduce-scatter.7.cloned.1.call-done = bf16[72,4608]{1,0:T(8,128)(2,1)} async-done(((bf16[1152,4608]{1,0:T(8,128)(2,1)}), bf16[72,4608]{1,0:T(8,128)(2,1)}) %reduce-scatter.7.cloned.1.call-update) | async-done | bytes 663568 | tf_op jit(solution)/shard_map/reduce_scatter | solution.py:32
  964.6 88.5 %reduce-scatter.9.cloned.1.call-done = bf16[72,4608]{1,0:T(8,128)(2,1)} async-done(((bf16[1152,4608]{1,0:T(8,128)(2,1)}), bf16[72,4608]{1,0:T(8,128)(2,1)}) %reduce-scatter.9.cloned.1.call-update) | async-done | bytes 663568 | tf_op jit(solution)/shard_map/reduce_scatter | solution.py:32
  1053.1 2.5 pad_maximum_fusion
  (34 shorter events, 0.1 us)
Async XLA Ops:
  7.2 62.4 %all-gather.13.cloned.1.call-start = ((), (), s32[]{:S(2)}) async-start(), calls=%async_computation.12 | async-start | bytes 11280384 | tf_op jit(solution)/shard_map/all_gather | solution.py:28
  9.7 118.0 %all-gather.15.cloned.1.call-start = ((), (), s32[]{:S(2)}) async-start(), calls=%async_computation.13 | async-start | bytes 11280384 | tf_op jit(solution)/shard_map/all_gather | solution.py:28
  12.2 173.6 %all-gather.17.cloned.1.call-start = ((), (), s32[]{:S(2)}) async-start(), calls=%async_computation.14 | async-start | bytes 11280384 | tf_op jit(solution)/shard_map/all_gather | solution.py:28
  14.8 229.0 %all-gather.19.cloned.1.call-start = ((), (), s32[]{:S(2)}) async-start(), calls=%async_computation.15 | async-start | bytes 11280384 | tf_op jit(solution)/shard_map/all_gather | solution.py:28
  15.4 287.0 %all-gather.23.cloned.1.call-start = ((), (), s32[]{:S(2)}) async-start(), calls=%async_computation.17 | async-start | bytes 11280384 | tf_op jit(solution)/shard_map/all_gather | solution.py:28
  15.9 345.0 %all-gather.21.cloned.1.call-start = ((), (), s32[]{:S(2)}) async-start(), calls=%async_computation.16 | async-start | bytes 11280384 | tf_op jit(solution)/shard_map/all_gather | solution.py:28
  16.5 797.3 %reduce-scatter.15.cloned.1.call-start = ((), (), s32[]{:S(2)}) async-start(), calls=%async_computation.10 | async-start | bytes 11280384 | tf_op jit(solution)/shard_map/reduce_scatter | solution.py:32
  26.5 0.6 copy-start.3
  27.1 100.5 %copy-start.5 = (f32[2048]{0:T(1024)}, f32[2048]{0:T(1024)S(1)}, u32[]{:S(2)}) copy-start(f32[2048]{0:T(1024)S(1)} %add_rsqrt_fusion.1) | copy-start | bytes 24580
  216.5 58.7 %copy-start.10 = (f32[2048]{0:T(1024)}, f32[2048]{0:T(1024)S(1)}, u32[]{:S(2)}) copy-start(f32[2048]{0:T(1024)S(1)} %get-tuple-element.20) | copy-start | bytes 24580
  216.5 265.1 %copy-start.8 = (f32[2048]{0:T(1024)}, f32[2048]{0:T(1024)S(1)}, u32[]{:S(2)}) copy-start(f32[2048]{0:T(1024)S(1)} %add_rsqrt_fusion) | copy-start | bytes 24580
  421.1 28.5 %copy-start = (bf16[2048,1152]{0,1:T(8,128)(2,1)S(1)}, bf16[2048,1152]{0,1:T(8,128)(2,1)}, u32[]{:S(2)}) copy-start(bf16[2048,1152]{0,1:T(8,128)(2,1)} %get-tuple-element.21) | copy-start | bytes 14155780
  449.6 32.0 %copy-start.2 = (bf16[2048,1152]{0,1:T(8,128)(2,1)}, bf16[2048,1152]{0,1:T(8,128)(2,1)S(1)}, u32[]{:S(2)}) copy-start(bf16[2048,1152]{0,1:T(8,128)(2,1)S(1)} %fusion.54) | copy-start | bytes 14155780
  449.6 32.0 %copy-start.11 = (f32[2048]{0:T(1024)S(1)}, f32[2048]{0:T(1024)}, u32[]{:S(2)}) copy-start(f32[2048]{0:T(1024)} %copy-done.10) | copy-start | bytes 24580
  526.3 287.5 %reduce-scatter.17.cloned.1.call-start = ((), (), s32[]{:S(2)}) async-start(), calls=%async_computation.11 | async-start | bytes 11280384 | tf_op jit(solution)/shard_map/reduce_scatter | solution.py:32
  563.8 252.5 %reduce-scatter.11.cloned.1.call-start = ((), (), s32[]{:S(2)}) async-start(), calls=%async_computation.8 | async-start | bytes 11280384 | tf_op jit(solution)/shard_map/reduce_scatter | solution.py:32
  563.9 53.0 %copy-start.6 = (f32[2048]{0:T(1024)S(1)}, f32[2048]{0:T(1024)}, u32[]{:S(2)}) copy-start(f32[2048]{0:T(1024)} %copy-done.5) | copy-start | bytes 24580
  645.5 0.7 copy-start.9
  645.5 230.4 %reduce-scatter.13.cloned.1.call-start = ((), (), s32[]{:S(2)}) async-start(), calls=%async_computation.9 | async-start | bytes 11280384 | tf_op jit(solution)/shard_map/reduce_scatter | solution.py:32
  674.9 289.7 %reduce-scatter.7.cloned.1.call-start = ((), (), s32[]{:S(2)}) async-start(), calls=%async_computation.6 | async-start | bytes 11280384 | tf_op jit(solution)/shard_map/reduce_scatter | solution.py:32
  703.6 349.5 %reduce-scatter.9.cloned.1.call-start = ((), (), s32[]{:S(2)}) async-start(), calls=%async_computation.7 | async-start | bytes 11280384 | tf_op jit(solution)/shard_map/reduce_scatter | solution.py:32
  732.5 28.5 %slice-start = ((s8[4718592]{0:T(1024)(128)(4,1)}), s8[524288]{0:T(1024)(128)(4,1)S(1)}, s32[]{:S(2)}) async-start(s8[4718592]{0:T(1024)(128)(4,1)} %bitcast.93), calls=%async_computation.18 | async-start | bytes 1048576
  732.5 28.5 %slice-start.1 = ((s8[4718592]{0:T(1024)(128)(4,1)}), s8[4194304]{0:T(1024)(128)(4,1)S(1)}, s32[]{:S(2)}) async-start(s8[4718592]{0:T(1024)(128)(4,1)} %bitcast.93), calls=%async_computation.19 | async-start | bytes 8388608
  761.0 32.2 %copy-start.1 = (bf16[2048,1152]{0,1:T(8,128)(2,1)}, bf16[2048,1152]{0,1:T(8,128)(2,1)S(1)}, u32[]{:S(2)}) copy-start(bf16[2048,1152]{0,1:T(8,128)(2,1)S(1)} %fusion.42) | copy-start | bytes 14155780
  761.0 32.2 %copy-start.4 = (f32[2048]{0:T(1024)S(1)}, f32[2048]{0:T(1024)}, u32[]{:S(2)}) copy-start(f32[2048]{0:T(1024)} %copy-done.3) | copy-start | bytes 24580
  761.0 32.3 %copy-start.7 = (f32[2048]{0:T(1024)S(1)}, f32[2048]{0:T(1024)}, u32[]{:S(2)}) copy-start(f32[2048]{0:T(1024)} %copy-done.5) | copy-start | bytes 24580
Sparse Core Ops, SparseCore 0:
  10.8 58.6 all-gather.12
  71.7 55.8 all-gather.14
  129.9 55.8 all-gather.16
  187.9 55.8 all-gather.18
  246.4 55.8 all-gather.22
  305.0 55.8 all-gather.20
  526.4 83.6 reduce-scatter.14
  615.0 83.6 reduce-scatter.16
  703.7 83.6 reduce-scatter.10
  792.2 83.6 reduce-scatter.12
  880.9 83.6 reduce-scatter.6
  969.4 83.6 reduce-scatter.8
